TPU v7x, 256 devices: a 8x8x2 block of a 8x8x16 slice. The times are simulated.
256 devices in a mesh: groups: 2 (over z), ep: 16 (over y, core), rep: 8 (over x).
Axes of the slice: x: 8, y: 8, z: 2, core: 2. Of those that a mesh axis runs over, the one named last changes fastest.
The devices are a block of a 8x8x16 slice.
Arguments:
- prompt_hidden: bfloat16 [8, 384, 2048], P('groups', 'ep'), parts along dimension 0, may hold values from -6 to 6
- decode_hidden: bfloat16 [4096, 8, 2048], P(('groups', 'ep'), 'rep'), parts along dimension 0, may hold values from -6 to 6
- queries: bfloat16 [4096, 8, 2048], P(('groups', 'ep'), None, 'rep'), parts along dimension 0, may hold values from -128 to 128
- attn_gain: float32 [2048], replicated, may hold values from 0.1 to 1.9
- key_value_weight: bfloat16 [2048, 1024], P(None, 'rep'), may hold values from -0.125 to 0.125
- out_weight: bfloat16 [2048, 2048], P('rep'), may hold values from -0.5 to 0.5
- moe_gain: float32 [2048], replicated, may hold values from 0.1 to 1.9
- gate_weight: bfloat16 [128, 2048, 768], P(('ep', 'rep')), may hold values from -0.125 to 0.125
- up_weight: bfloat16 [128, 2048, 768], P(('ep', 'rep')), may hold values from -0.125 to 0.125
- down_weight: bfloat16 [128, 768, 2048], P(('ep', 'rep')), may hold values from -0.21875 to 0.21875
- expert_table: int32 [151936], replicated, may hold values from 0 to 127, as said below
- token_ids: int32 [2048, 8], P('ep', 'rep'), may hold values from 0 to 151935, as said below
- prompt_lengths: int32 [8], P('groups'), parts along dimension 0, may hold values from 1 to 384, 960 in all
Outputs:
- layer_out: bfloat16 [4096, 8, 2048], P(('groups', 'ep'), 'rep'), parts along dimension 0
There are 2 independent parts, one for each index of `groups`. A program takes and returns all parts, laid end to end along the dimension named above; an argument that names none is the same for every part. Nothing has to cross between parts.
Inputs may be any that keep to these rules, and one draw needn't show every extreme that they name: `expert_table`: each expert is the value of exactly 1187 entries. `token_ids`: a device holds the 128 sequences of its index of ep at 8 // 8 steps of its index of rep; of these tokens at most 2 go to one expert; in every draw one expert receives exactly 2 from every device. `prompt_lengths`: the lengths of a group sum to 960 and the longest is 384.
All inputs are finite; a program needn't handle non-finite values.
Results may differ from a plain program's by a relative error of at most 0.017.
The roundings to bfloat16 on the way count: a program that leaves them out, or rounds other values in their place, can miss the bound.
Values may be sent and summed in bfloat16 or wider, within the bound.
A program may use at most 128 MiB of HBM per device.

v0:
```python
import math
import jax
import jax.numpy as jnp
from jax import lax
from jax.sharding import PartitionSpec as P

HEAD_DIM = 128
QUERY_HEADS = 16
KEY_VALUE_HEADS = 4
GROUP_PROMPTS = 4
CAP = 2
EPS = 1e-06
THETA = 1000000.0


def in_one_piece(arrays, axis, dim, along):
    both = jnp.concatenate(arrays, axis=along)
    filled, at, outs = (lax.all_gather(both, axis, axis=dim, tiled=True), 0, [])
    for a in arrays:
        outs.append(lax.slice_in_dim(filled, at, at + a.shape[along], axis=along))
        at += a.shape[along]
    return tuple(outs)


def swapped(block, axis, bit):
    count = lax.axis_size(axis)
    route = []
    for low in range(count):
        high = low | 1 << bit
        if high != low and high < count:
            route += [(low, high), (high, low)]
    return lax.ppermute(block, axis, route)


def rms_scale(hidden, gain_vec):
    widened = hidden.astype(jnp.float32)
    mean_sq = jnp.mean(widened * widened, axis=-1, keepdims=True)
    return widened * lax.rsqrt(mean_sq + EPS) * gain_vec


def rotate(vectors, positions):
    half_dim = vectors.shape[-1] // 2
    inverse_freq = jnp.exp(
        jnp.arange(half_dim, dtype=jnp.float32) * (-2.0 * math.log(THETA) / vectors.shape[-1])
    )
    angles = positions[..., None] * inverse_freq
    cosine = jnp.cos(angles)
    sine_part = jnp.sin(angles)
    first_half = vectors[..., :half_dim]
    second_half = vectors[..., half_dim:]
    return jnp.concatenate(
        [
            first_half * cosine - second_half * sine_part,
            second_half * cosine + first_half * sine_part,
        ],
        axis=-1,
    )


def expert_apply(tokens, gate_weight, up_weight, down_weight):
    flat_rows = tokens.reshape(-1, tokens.shape[-1])
    gate_proj = jnp.dot(flat_rows, gate_weight[0], preferred_element_type=jnp.float32)
    up_proj = jnp.dot(flat_rows, up_weight[0], preferred_element_type=jnp.float32)
    hidden = (jax.nn.silu(gate_proj) * up_proj).astype(jnp.bfloat16)
    return (
        jnp.dot(hidden, down_weight[0], preferred_element_type=jnp.float32)
        .astype(jnp.bfloat16)
        .reshape(tokens.shape)
    )


def local(
    prompt_hidden,
    decode_hidden,
    queries,
    attn_gain,
    key_value_weight,
    out_weight,
    moe_gain,
    gate_weight,
    up_weight,
    down_weight,
    expert_table,
    token_ids,
    prompt_lengths,
):
    full_hidden = lax.all_gather(decode_hidden, "rep", axis=1, tiled=True)
    sequences_local, steps_total, model_width = full_hidden.shape
    prompt_length_local = prompt_hidden.shape[1]
    qh_dev = queries.shape[2] // HEAD_DIM
    group_count = QUERY_HEADS // KEY_VALUE_HEADS
    ep_count = lax.axis_size("ep")
    rep_count = lax.axis_size("rep")
    ep_index = lax.axis_index("ep")
    rep_index = lax.axis_index("rep")
    seq_total = sequences_local * ep_count
    samples = seq_total // GROUP_PROMPTS
    score_scale = HEAD_DIM ** (-0.5)
    step_rows = steps_total // rep_count
    blocks = key_value_weight.shape[1] // HEAD_DIM

    def own_columns(hidden, positions):
        leading = hidden.shape[:-1]
        normed = rms_scale(hidden, attn_gain).astype(jnp.bfloat16)
        projected = jnp.dot(
            normed.reshape(-1, model_width), key_value_weight, preferred_element_type=jnp.float32
        )
        projected = projected.reshape(leading + (blocks, HEAD_DIM))
        block_ids = rep_index * blocks + jnp.arange(blocks, dtype=jnp.int32)
        is_key = (block_ids % 2 == 0)[:, None]
        turned = rotate(projected, positions[..., None])
        return (
            jnp.where(is_key, turned, projected)
            .astype(jnp.bfloat16)
            .reshape(leading + (blocks * HEAD_DIM,))
        )

    key_pos = ep_index * prompt_length_local + jnp.arange(prompt_length_local, dtype=jnp.int32)
    prompt_pos = jnp.broadcast_to(
        key_pos.astype(jnp.float32)[None, :], (GROUP_PROMPTS, prompt_length_local)
    )
    own_seqs = ep_index * sequences_local + jnp.arange(sequences_local, dtype=jnp.int32)
    own_prompt = own_seqs // samples
    own_lengths = jnp.take(prompt_lengths, own_prompt)
    decode_pos = (
        own_lengths[:, None].astype(jnp.float32)
        + jnp.arange(steps_total, dtype=jnp.float32)[None, :]
    )
    prompt_part = own_columns(prompt_hidden, prompt_pos)
    decode_part = own_columns(full_hidden, decode_pos)
    prompt_hot = own_prompt[:, None] == jnp.arange(GROUP_PROMPTS, dtype=jnp.int32)[None, :]
    partner_prompt, partner_decode = swapped((prompt_part, decode_part), "rep", 0)
    holds_key = rep_index % 2 == 0
    prompt_columns = jnp.where(
        holds_key,
        jnp.concatenate([prompt_part, partner_prompt], axis=2),
        jnp.concatenate([partner_prompt, prompt_part], axis=2),
    )
    decode_columns = jnp.where(
        holds_key,
        jnp.concatenate([decode_part, partner_decode], axis=2),
        jnp.concatenate([partner_decode, decode_part], axis=2),
    )
    heads_here = 1
    head_base = rep_index // 2
    prompt_key_value = prompt_columns.reshape(
        GROUP_PROMPTS, prompt_length_local, heads_here, 2, HEAD_DIM
    )
    decode_key_value = decode_columns.reshape(sequences_local, steps_total, heads_here, 2, HEAD_DIM)
    prompt_keys = prompt_key_value[:, :, :, 0, :]
    prompt_values = prompt_key_value[:, :, :, 1, :]
    decode_keys = decode_key_value[:, :, :, 0, :]
    decode_values = decode_key_value[:, :, :, 1, :]
    query_matrix = queries.reshape(sequences_local, steps_total, qh_dev, HEAD_DIM)
    head_pick = (
        rep_index * qh_dev + jnp.arange(qh_dev, dtype=jnp.int32)
    ) // group_count - head_base
    own_keys = jnp.take(decode_keys, head_pick, axis=2)
    own_values = jnp.take(decode_values, head_pick, axis=2)
    self_scores = (
        jnp.einsum("sthd,suhd->sthu", query_matrix, own_keys, preferred_element_type=jnp.float32)
        * score_scale
    )
    self_mask = (
        jnp.arange(steps_total, dtype=jnp.int32)[None, :]
        <= jnp.arange(steps_total, dtype=jnp.int32)[:, None]
    )[None, :, None, :]
    self_scores = jnp.where(self_mask, self_scores, -1e30)
    self_top = jnp.max(self_scores, axis=-1)
    start_weights = jnp.where(self_mask, jnp.exp(self_scores - self_top[..., None]), 0.0)
    pieces = in_one_piece((prompt_keys, prompt_values), "ep", 1, 0)
    row_top = self_top
    row_total = jnp.sum(start_weights, axis=-1)
    weighted = jnp.einsum(
        "sthu,suhd->sthd",
        start_weights.astype(jnp.bfloat16),
        own_values,
        preferred_element_type=jnp.float32,
    )
    piece_keys = jnp.take(pieces[0], head_pick, axis=2)
    piece_values = jnp.take(pieces[1], head_pick, axis=2)
    piece_len = piece_keys.shape[1]
    valid = jnp.arange(piece_len, dtype=jnp.int32)[None, :] < prompt_lengths[:, None]
    key_mask = prompt_hot[:, None, None, :, None] & valid[None, None, None, :, :]
    scores = (
        jnp.einsum("sthd,pnhd->sthpn", query_matrix, piece_keys, preferred_element_type=jnp.float32)
        * score_scale
    )
    scores = jnp.where(key_mask, scores, -1e30)
    new_top = jnp.maximum(row_top, jnp.max(scores, axis=(-2, -1)))
    decay = jnp.exp(row_top - new_top)
    weights = jnp.where(key_mask, jnp.exp(scores - new_top[..., None, None]), 0.0)
    weighted = weighted * decay[..., None] + jnp.einsum(
        "sthpn,pnhd->sthd",
        weights.astype(jnp.bfloat16),
        piece_values,
        preferred_element_type=jnp.float32,
    )
    row_top, row_total, weighted = (
        new_top,
        row_total * decay + jnp.sum(weights, axis=(-2, -1)),
        weighted,
    )
    attended = weighted / row_total[..., None]
    heads_out = attended.reshape(sequences_local, steps_total, qh_dev * HEAD_DIM).astype(
        jnp.bfloat16
    )
    by_step = jnp.swapaxes(heads_out, 0, 1)
    attn_sum = jnp.swapaxes(
        lax.psum_scatter(
            jnp.dot(
                by_step.reshape(-1, by_step.shape[-1]),
                out_weight,
                preferred_element_type=jnp.float32,
            )
            .reshape(step_rows * lax.axis_size("rep"), sequences_local, model_width)
            .astype(jnp.bfloat16),
            "rep",
            scatter_dimension=0,
            tiled=True,
        ).astype(jnp.float32),
        0,
        1,
    )
    attn_mixed = (decode_hidden.astype(jnp.float32) + attn_sum).astype(jnp.bfloat16)
    row_count = sequences_local * step_rows
    normed = rms_scale(attn_mixed, moe_gain).astype(jnp.bfloat16).reshape(row_count, model_width)
    chosen = jnp.take(expert_table, token_ids.reshape(row_count))
    device_count = ep_count * rep_count
    slot_total = device_count * CAP
    same_expert = chosen[:, None] == chosen[None, :]
    before = jnp.arange(row_count)[None, :] < jnp.arange(row_count)[:, None]
    slot_rank = jnp.sum((same_expert & before).astype(jnp.int32), axis=1)
    destination = chosen * CAP + slot_rank
    send_pick = (jnp.arange(slot_total, dtype=jnp.int32)[:, None] == destination[None, :]).astype(
        jnp.bfloat16
    )
    outgoing = (
        jnp.dot(send_pick, normed, preferred_element_type=jnp.float32)
        .astype(jnp.bfloat16)
        .reshape(device_count, CAP, model_width)
    )
    served = expert_apply(
        lax.all_to_all(outgoing, ("ep", "rep"), split_axis=0, concat_axis=0, tiled=True),
        gate_weight,
        up_weight,
        down_weight,
    )
    returned = lax.all_to_all(served, ("ep", "rep"), split_axis=0, concat_axis=0, tiled=True)
    moe_out = lax.dot_general(
        send_pick,
        returned.reshape(slot_total, model_width),
        (((0,), (0,)), ((), ())),
        preferred_element_type=jnp.float32,
    )
    layer_out = (
        attn_mixed.astype(jnp.float32) + moe_out.reshape(sequences_local, step_rows, model_width)
    ).astype(jnp.bfloat16)
    return layer_out


def solution(mesh):
    placed = (
        P("groups", "ep", None),
        P(("groups", "ep"), "rep", None),
        P(("groups", "ep"), None, "rep"),
        P(),
        P(None, "rep"),
        P("rep", None),
        P(),
        P(("ep", "rep"), None, None),
        P(("ep", "rep"), None, None),
        P(("ep", "rep"), None, None),
        P(),
        P("ep", "rep"),
        P("groups"),
    )
    return jax.shard_map(
        local,
        mesh=mesh,
        in_specs=placed,
        out_specs=P(("groups", "ep"), "rep", None),
        check_vma=False,
    )
```

profile of v0, /device:TPU:513, one launch (start us, length us, event | category | flops | bytes accessed | tf_op | source)
XLA Modules:
  0.0 316.9 jit_solution(7113456730417869289)
XLA Ops:
  6.6 0.7 all-gather.2.cloned.1.call-update
  7.4 1.2 fusion.39
  8.7 1.2 fusion.41
  9.8 1.3 fusion.110
  11.4 2.3 collective-permute-start.1
  13.7 1.5 fusion.109
  15.1 2.5 fusion.100
  18.2 0.7 iota_compare_fusion.4
  18.9 0.7 iota_add_fusion
  19.6 0.9 broadcast_and_fusion
  21.3 35.0 %all_gather.7 = bf16[8,384,1,128]{3,0,2,1:T(8,128)(2,1)S(1)} all-gather(bf16[8,24,1,128]{3,0,2,1:T(8,128)(2,1)S(1)} %copy.139), channel_id=1, replica_groups=mesh['groups'=2,'ep'=16,'rep'=8] {'ep'}, dimensions={1}, use_global_device_ids=true | all-gather | bytes 835584 | tf_op jit(solution)/shard_map/all_gather | solution.py:18
  56.6 0.8 copy.140
  57.3 26.0 %all-gather.2.cloned.1.call-done = bf16[128,8,2048]{2,0,1:T(8,128)(2,1)} async-done(((bf16[128,1,2048]{2,0,1:T(8,128)(2,1)}), bf16[128,8,2048]{2,0,1:T(8,128)(2,1)}) %all-gather.2.cloned.1.call-update) | async-done | bytes 4194320 | tf_op jit(solution)/shard_map/all_gather | solution.py:87
  83.4 5.1 %fusion.3 = f32[128,8]{1,0:T(8,128)} fusion(bf16[128,8,2048]{2,0,1:T(8,128)(2,1)} %all-gather.2.cloned.1.call-done), kind=kLoop, calls=%fused_computation.8 | loop fusion | flops 6290432 | bytes 4198400 | tf_op jit(solution)/shard_map/reduce_sum | solution.py:37
  88.5 0.9 copy.131
  89.4 0.7 copy.132
  90.2 5.0 %fusion.7 = f32[1024,128]{1,0:T(8,128)S(1)} fusion(bf16[2048,128]{1,0:T(8,128)(2,1)} %param.21, f32[2048]{0:T(1024)S(1)} %copy-done.10, f32[128,8]{1,0:T(8,128)} %copy.132, bf16[128,8,2048]{2,0,1:T(8,128)(2,1)} %all-gather.2.cloned.1.call-done), kind=kOutput, calls=%fused_computation.12 | convolution fusion | flops 545259520 | bytes 5255168 | tf_op jit(solution)/shard_map/dot_general | solution.py:105
  95.2 2.4 fusion.56
  98.1 5.7 %fusion = (f32[128,8,2]{0,1,2:T(8,128)S(1)}, f32[2,4,384,128,8]{3,2,4,1,0:T(8,128)}) fusion(pred[128,4,384]{0,2,1:T(8,128)(4,1)S(1)} %copy-done.3, bf16[128,8,2,128,1]{3,1,2,0,4:T(8,128)(2,1)S(1)} %bitcast.168, pred[2]{0:T(512)(128)(4,1)S(1)} %copy-done.14, bf16[4,384,128]{2,1,0:T(8,128)(2,1)S(1)} %copy-done.6), kind=kOutput, calls=%fused_computation.3 | convolution fusion | flops 815134720 | bytes 13705218 | tf_op jit(solution)/shard_map/sthd,pnhd->sthpn/dot_general | solution.py:186
  103.8 0.8 copy.145
  105.3 0.8 slice_bitcast_fusion.3
  106.0 1.5 fusion.64
  107.5 1.6 copy.135
  109.2 0.7 fusion.89
  109.9 1.9 fusion.95
  111.8 9.7 %fusion.2 = (bf16[128,8,2,4,384]{0,4,1,3,2:T(8,128)(2,1)}, f32[128,8,2]{0,1,2:T(8,128)S(1)}) fusion(f32[2,4,384,128,8]{3,2,4,1,0:T(8,128)} %get-tuple-element.28, f32[128,8,2]{0,1,2:T(8,128)S(1)} %copy_maximum_fusion, pred[128,4,384]{0,2,1:T(8,128)(4,1)} %broadcast_and_fusion), kind=kLoop, calls=%fused_computation.7 | loop fusion | flops 18872320 | bytes 19087360 | tf_op jit(solution)/shard_map/convert_element_type | solution.py:195
  121.5 9.0 %copy.146 = bf16[128,8,2,4,384]{4,1,3,2,0:T(8,128)(2,1)} copy(bf16[128,8,2,4,384]{0,4,1,3,2:T(8,128)(2,1)} %get-tuple-element.9) | data formatting | bytes 12582912 | tf_op jit(solution)/shard_map/convert_element_type | solution.py:195
  130.6 1.4 fusion.97
  131.9 1.5 copy.144
  133.4 1.9 copy.138
  135.4 1.5 copy.149
  136.8 1.8 fusion.25
  138.7 1.2 copy-done.1
  139.9 2.6 fusion.33
  142.6 3.2 %convolution_convert_fusion = bf16[8,128,2048]{2,1,0:T(8,128)(2,1)} fusion(bf16[256,2048]{1,0:T(8,128)(2,1)S(1)} %copy-done.2, bf16[8,128,256]{2,0,1:T(8,128)(2,1)S(1)} %fusion.33), kind=kOutput, calls=%fused_computation.15 | convolution fusion | flops 1075838976 | bytes 5767168 | tf_op jit(solution)/shard_map/dot_general | solution.py:211
  145.9 2.1 gather_fusion
  148.2 54.3 %reduce-scatter.2.cloned.1.call-done = bf16[1,128,2048]{2,1,0:T(8,128)(2,1)} async-done(((bf16[8,128,2048]{2,1,0:T(8,128)(2,1)}), bf16[1,128,2048]{2,1,0:T(8,128)(2,1)}) %reduce-scatter.2.cloned.1.call-update) | async-done | bytes 524304 | tf_op jit(solution)/shard_map/reduce_scatter | solution.py:210
  202.5 1.5 fusion.34
  203.9 2.7 convolution_convert_fusion.1
  206.7 2.5 reshape.407
  209.2 42.8 %all_to_all.10 = bf16[128,2,2048]{2,1,0:T(2,128)(2,1)} all-to-all(bf16[128,2,2048]{2,1,0:T(2,128)(2,1)} %reshape.407), channel_id=1, replica_groups=mesh['groups'=2,'ep'=16,'rep'=8] {'ep','rep'}, dimensions={0} | all-to-all | bytes 2097152 | tf_op jit(solution)/shard_map/all_to_all | solution.py:244
  252.0 2.2 reshape.408
  254.3 4.1 %fusion.16 = f32[256,768]{1,0:T(8,128)} fusion(bf16[256,2048]{1,0:T(8,128)(2,1)} %reshape.408, bf16[1,2048,768]{2,1,0:T(8,128)(2,1)} %param.24), kind=kOutput, calls=%fused_computation.21 | convolution fusion | flops 805306368 | bytes 4980736 | tf_op jit(solution)/shard_map/dot_general | solution.py:62
  258.3 5.5 %fusion.18 = bf16[256,2048]{1,0:T(8,128)(2,1)} fusion(bf16[1,768,2048]{2,1,0:T(8,128)(2,1)S(1)} %copy-done, bf16[256,2048]{1,0:T(8,128)(2,1)} %reshape.408, bf16[1,2048,768]{2,1,0:T(8,128)(2,1)} %param.25, f32[256,768]{1,0:T(8,128)} %fusion.16), kind=kOutput, calls=%fused_computation.24 | convolution fusion | flops 1612316672 | bytes 9175040 | tf_op jit(solution)/shard_map/dot_general | solution.py:66
  263.9 2.5 reshape.409
  266.4 38.7 %all_to_all.11 = bf16[128,2,2048]{2,1,0:T(2,128)(2,1)} all-to-all(bf16[128,2,2048]{2,1,0:T(2,128)(2,1)} %reshape.409), channel_id=1, replica_groups=mesh['groups'=2,'ep'=16,'rep'=8] {'ep','rep'}, dimensions={0} | all-to-all | bytes 2097152 | tf_op jit(solution)/shard_map/all_to_all | solution.py:249
  305.1 2.2 reshape.410
  307.3 2.7 fusion.22
  (64 shorter events, 3.3 us)
Async XLA Ops:
  6.5 251.8 %copy-start = (bf16[1,768,2048]{2,1,0:T(8,128)(2,1)S(1)}, bf16[1,768,2048]{2,1,0:T(8,128)(2,1)}, u32[]{:S(2)}) copy-start(bf16[1,768,2048]{2,1,0:T(8,128)(2,1)} %param.26) | copy-start | bytes 9437188
  6.6 83.6 %copy-start.10 = (f32[2048]{0:T(1024)S(1)}, f32[2048]{0:T(1024)}, u32[]{:S(2)}) copy-start(f32[2048]{0:T(1024)} %param.20) | copy-start | bytes 24580
  6.6 76.8 %all-gather.2.cloned.1.call-start = ((), (), s32[]{:S(2)}) async-start(), calls=%async_computation.3 | async-start | bytes 4718592 | tf_op jit(solution)/shard_map/all_gather | solution.py:87
  7.3 195.2 %reduce-scatter.2.cloned.1.call-start = ((), (), s32[]{:S(2)}) async-start(), calls=%async_computation.4 | async-start | bytes 4718592 | tf_op jit(solution)/shard_map/reduce_scatter | solution.py:210
  7.4 4.0 %copy-start.12 = (f32[64]{0:T(128)}, f32[64]{0:T(128)S(1)}, u32[]{:S(2)}) copy-start(f32[64]{0:T(128)S(1)} %multiply_exponential_fusion) | copy-start | bytes 772
  11.4 9.7 %collective-permute-start.1 = (bf16[4,24,128]{2,1,0:T(8,128)(2,1)S(1)}, bf16[4,24,128]{2,1,0:T(8,128)(2,1)S(1)}, u32[]{:S(2)}, u32[]{:S(2)}) collective-permute-start(bf16[4,24,128]{2,1,0:T(8,128)(2,1)S(1)} %fusion.94), channel_id=1, source_target_pairs={{0,1},{1,0},{2,3},{3,2},{4,5},{5,4},{6,7},{7,6},{8,9},{9,8},{10,11... | collective-permute-start | bytes 73736 | tf_op jit(solution)/shard_map/ppermute | solution.py:32
  90.2 5.0 %copy-start.7 = (f32[128,8]{1,0:T(8,128)S(1)}, f32[128,8]{1,0:T(8,128)}, u32[]{:S(2)}) copy-start(f32[128,8]{1,0:T(8,128)} %iota_add_fusion) | copy-start | bytes 12292
  90.2 5.0 %copy-start.13 = (f32[64]{0:T(128)S(1)}, f32[64]{0:T(128)}, u32[]{:S(2)}) copy-start(f32[64]{0:T(128)} %copy-done.12) | copy-start | bytes 772
  90.2 7.9 %copy-start.3 = (pred[128,4,384]{0,2,1:T(8,128)(4,1)S(1)}, pred[128,4,384]{0,2,1:T(8,128)(4,1)}, u32[]{:S(2)}) copy-start(pred[128,4,384]{0,2,1:T(8,128)(4,1)} %broadcast_and_fusion) | copy-start | bytes 589828
  90.2 7.9 %copy-start.4 = (bf16[128,8,256]{2,1,0:T(8,128)(2,1)S(1)}, bf16[128,8,256]{2,1,0:T(8,128)(2,1)}, u32[]{:S(2)}) copy-start(bf16[128,8,256]{2,1,0:T(8,128)(2,1)} %param.19) | copy-start | bytes 1572868
  90.2 7.9 %copy-start.6 = (bf16[4,384,128]{2,1,0:T(8,128)(2,1)S(1)}, bf16[4,384,128]{2,1,0:T(8,128)(2,1)}, u32[]{:S(2)}) copy-start(bf16[4,384,128]{2,1,0:T(8,128)(2,1)} %copy.140) | copy-start | bytes 1179652
  90.2 7.9 %copy-start.14 = (pred[2]{0:T(512)(128)(4,1)S(1)}, pred[2]{0:T(512)(128)(4,1)}, u32[]{:S(2)}) copy-start(pred[2]{0:T(512)(128)(4,1)} %compare_and_fusion) | copy-start | bytes 10
  97.8 7.3 %collective-permute-start = (bf16[128,8,128]{2,1,0:T(8,128)(2,1)S(1)}, bf16[128,8,128]{2,1,0:T(8,128)(2,1)S(1)}, u32[]{:S(2)}, u32[]{:S(2)}) collective-permute-start(bf16[128,8,128]{2,1,0:T(8,128)(2,1)S(1)} %fusion.61), channel_id=1, source_target_pairs={{0,1},{1,0},{2,3},{3,2},{4,5},{5,4},{6,7},{7,6},{8,9},{9,8},{10,11... | collective-permute-start | bytes 786440 | tf_op jit(solution)/shard_map/ppermute | solution.py:32
  103.8 8.0 %copy-start.9 = (f32[128,8,2]{0,1,2:T(8,128)}, f32[128,8,2]{0,1,2:T(8,128)S(1)}, u32[]{:S(2)}) copy-start(f32[128,8,2]{0,1,2:T(8,128)S(1)} %get-tuple-element.27) | copy-start | bytes 24580
  130.6 8.1 %copy-start.5 = (bf16[4,384,128]{2,1,0:T(8,128)(2,1)S(1)}, bf16[4,384,128]{2,1,0:T(8,128)(2,1)}, u32[]{:S(2)}) copy-start(bf16[4,384,128]{2,1,0:T(8,128)(2,1)} %copy.145) | copy-start | bytes 1179652
  136.8 3.1 copy-start.1
  136.8 3.1 copy-start.8
  139.9 2.6 copy-start.2
  142.6 3.3 %copy-start.15 = (s32[128,1]{0,1:T(1,128)S(1)}, s32[128,1]{0,1:T(1,128)}, u32[]{:S(2)}) copy-start(s32[128,1]{0,1:T(1,128)} %param.28) | copy-start | bytes 1540
  142.6 61.4 %copy-start.11 = (f32[2048]{0:T(1024)S(1)}, f32[2048]{0:T(1024)}, u32[]{:S(2)}) copy-start(f32[2048]{0:T(1024)} %param.23) | copy-start | bytes 24580
Sparse Core Ops, SparseCore 0:
  9.1 74.2 all-gather.1
  146.0 56.4 reduce-scatter.1
where the time goes:
time: 318 us; the launch traced here: 317 us
  blocking collectives  116 us (36%)
  waiting for transfers between devices  81.6 us (26%)
  matrix products  36.1 us (11%)
  local copies, waits for them, and re-layouts  34.3 us (11%)
  other arithmetic  31.9 us (10%)
  between operations  13.8 us (4%)
    reduce_scatter x1, waiting for transfers between devices, local(): lax.psum_scatter(jnp.dot(by_step.reshape(-1, by_step.shape[-1]), out_weig...  54.3 us
    all_to_all x1, blocking collectives, local(): lax.all_to_all(outgoing, ('ep', 'rep'), split_axis=0, concat_axis=0, tile...  42.8 us
    all_to_all x1, blocking collectives, local(): lax.all_to_all(served, ('ep', 'rep'), split_axis=0, concat_axis=0, tiled=...  38.7 us
    all_gather x1, blocking collectives, in_one_piece(): filled, at, outs = (lax.all_gather(both, axis, axis=dim, tiled=True), 0, [])  35 us
    all_gather x1, waiting for transfers between devices, local(): full_hidden = lax.all_gather(decode_hidden, 'rep', axis=1, tiled=True)  26 us
    convert_element_type x1, other arithmetic, local(): weights.astype(jnp.bfloat16)  9.72 us
    convert_element_type x1, local copies, waits for them, and re-layouts, local(): weights.astype(jnp.bfloat16)  9.02 us
    reduce_sum x3, other arithmetic, rms_scale(): mean_sq = jnp.mean(widened * widened, axis=-1, keepdims=True)  7.81 us
  transfers between devices with their start and end apart: 4, of which 3 were waited for; matrix products, arithmetic and copies ran while one was open for 7% of the time, Pallas kernels for 0%

commit v1 on v0

--- a/solution.py
+++ b/solution.py
@@ -84,7 +84,9 @@
     token_ids,
     prompt_lengths,
 ):
-    full_hidden = lax.all_gather(decode_hidden, "rep", axis=1, tiled=True)
+    full_hidden = jnp.concatenate(
+        lax.all_to_all(jnp.stack([decode_hidden] * lax.axis_size("rep")), "rep", 0, 0), axis=1
+    )
     sequences_local, steps_total, model_width = full_hidden.shape
     prompt_length_local = prompt_hidden.shape[1]
     qh_dev = queries.shape[2] // HEAD_DIM

time: 318 us -> 376 us (1.18)
  waiting for transfers between devices: 81.6 us -> 129 us
  blocking collectives: 116 us -> 126 us
  starting transfers between devices: 2.67 us -> 9.87 us
  other arithmetic: 31.9 us -> 25.5 us
    ppermute x2, waiting for transfers between devices: 0.47 us -> 68.7 us  [swapped(): return lax.ppermute(block, axis, route)]
    all_gather x1 -> x0, waiting for transfers between devices: 26 us -> none  [local(): full_hidden = lax.all_gather(decode_hidden, 'rep', axis=1, tiled=True)]
    all_gather x1, blocking collectives: 35 us -> 44.4 us  [in_one_piece(): filled, at, outs = (lax.all_gather(both, axis, axis=dim, tiled=True), 0, [])]
    all_to_all x0 -> x1, starting transfers between devices: none -> 7.99 us  [local(): lax.all_to_all(jnp.stack([decode_hidden] * lax.axis_size('rep')), 'rep',...]
    reduce_scatter x1, waiting for transfers between devices: 54.3 us -> 60.2 us  [local(): lax.psum_scatter(jnp.dot(by_step.reshape(-1, by_step.shape[-1]), out_weig...]
  transfers between devices with their start and end apart: 4 -> 4, of which waited for: 3 -> 3; matrix products, arithmetic and copies ran while one was open for 7% -> 5% of each run, Pallas kernels for 0% -> 0%
where the time goes in v1:
time: 376 us; the launch traced here: 375 us
  waiting for transfers between devices  129 us (34%)
  blocking collectives  126 us (34%)
  local copies, waits for them, and re-layouts  35.9 us (10%)
  matrix products  35.6 us (9%)
  other arithmetic  25.5 us (7%)
  between operations  13.8 us (4%)
  starting transfers between devices  9.87 us (3%)
    ppermute x2, waiting for transfers between devices, swapped(): return lax.ppermute(block, axis, route)  68.7 us
    reduce_scatter x1, waiting for transfers between devices, local(): lax.psum_scatter(jnp.dot(by_step.reshape(-1, by_step.shape[-1]), out_weig...  60.2 us
    all_gather x1, blocking collectives, in_one_piece(): filled, at, outs = (lax.all_gather(both, axis, axis=dim, tiled=True), 0, [])  44.4 us
    all_to_all x1, blocking collectives, local(): lax.all_to_all(outgoing, ('ep', 'rep'), split_axis=0, concat_axis=0, tile...  42.8 us
    all_to_all x1, blocking collectives, local(): lax.all_to_all(served, ('ep', 'rep'), split_axis=0, concat_axis=0, tiled=...  38.7 us
    convert_element_type x1, other arithmetic, local(): weights.astype(jnp.bfloat16)  9.69 us
    convert_element_type x1, local copies, waits for them, and re-layouts, local(): weights.astype(jnp.bfloat16)  8.98 us
    all_to_all x1, starting transfers between devices, local(): lax.all_to_all(jnp.stack([decode_hidden] * lax.axis_size('rep')), 'rep',...  7.99 us
  transfers between devices with their start and end apart: 4, of which 3 were waited for; matrix products, arithmetic and copies ran while one was open for 5% of the time, Pallas kernels for 0%

profile of v1, /device:TPU:513, one launch (start us, length us, event | category | flops | bytes accessed | tf_op | source)
XLA Modules:
  0.0 375.5 jit_solution(16706068130267029751)
XLA Ops:
  6.6 3.7 stack.2
  10.2 8.0 %all-to-all-start = ((bf16[8,128,1,2048]{3,1,2,0:T(8,128)(2,1)}), bf16[8,128,1,2048]{3,1,2,0:T(8,128)(2,1)}, u32[]{:S(2)}, u32[]{:S(2)}) async-start(bf16[8,128,1,2048]{3,1,2,0:T(8,128)(2,1)} %stack.2), calls=%async_computation | async-start | bytes 8388608 | tf_op jit(solution)/shard_map/all_to_all | solution.py:88
  18.7 1.3 fusion.110
  20.3 1.5 collective-permute-start.1
  21.8 0.7 fusion.109
  22.4 2.5 fusion.100
  25.0 0.6 iota_compare_fusion.5
  25.6 0.7 iota_add_fusion
  26.3 1.0 broadcast_and_fusion
  27.3 0.6 compare_and_fusion
  27.9 67.7 %collective-permute-done.1 = bf16[4,24,128]{2,1,0:T(8,128)(2,1)S(1)} collective-permute-done((bf16[4,24,128]{2,1,0:T(8,128)(2,1)S(1)}, bf16[4,24,128]{2,1,0:T(8,128)(2,1)S(1)}, u32[]{:S(2)}, u32[]{:S(2)}) %collective-permute-start.1) | collective-permute-done | bytes 24608 | tf_op jit(solution)/shard_map/ppermute | solution.py:32
  95.8 44.4 %all_gather.3 = bf16[8,384,1,128]{3,0,2,1:T(8,128)(2,1)S(1)} all-gather(bf16[8,24,1,128]{3,0,2,1:T(8,128)(2,1)S(1)} %copy.138), channel_id=1, replica_groups=mesh['groups'=2,'ep'=16,'rep'=8] {'ep'}, dimensions={1}, use_global_device_ids=true | all-gather | bytes 835584 | tf_op jit(solution)/shard_map/all_gather | solution.py:18
  140.4 0.8 copy.139
  141.2 5.1 %fusion.6 = f32[8,128]{0,1:T(8,128)} fusion(bf16[8,128,1,2048]{3,1,2,0:T(8,128)(2,1)} %all-to-all-done), kind=kLoop, calls=%fused_computation.11 | loop fusion | flops 6290432 | bytes 4198400 | tf_op jit(solution)/shard_map/reduce_sum | solution.py:37
  146.4 0.9 copy.130
  147.3 0.8 copy.131
  148.0 0.9 rsqrt.28
  149.0 4.9 %fusion.7 = f32[1024,128]{1,0:T(8,128)S(1)} fusion(bf16[2048,128]{1,0:T(8,128)(2,1)} %param.21, f32[2048]{0:T(1024)S(1)} %copy-done.11, f32[1024]{0:T(1024)S(1)} %rsqrt.28, bf16[8,128,1,2048]{3,1,2,0:T(8,128)(2,1)} %all-to-all-done), kind=kOutput, calls=%fused_computation.12 | convolution fusion | flops 545259520 | bytes 5255168 | tf_op jit(solution)/shard_map/dot_general | solution.py:107
  154.0 2.4 fusion.56
  156.5 0.3 collective-permute-start
  156.9 5.8 %fusion = (f32[128,8,2]{0,1,2:T(8,128)S(1)}, f32[2,4,384,128,8]{3,2,4,1,0:T(8,128)}) fusion(pred[128,4,384]{0,2,1:T(8,128)(4,1)S(1)} %copy-done.4, bf16[128,8,2,128,1]{3,1,2,0,4:T(8,128)(2,1)S(1)} %bitcast.180, pred[2]{0:T(512)(128)(4,1)S(1)} %copy-done.16, bf16[4,384,128]{2,1,0:T(8,128)(2,1)S(1)} %copy-done.7), kind=kOutput, calls=%fused_computation.3 | convolution fusion | flops 815134720 | bytes 13705218 | tf_op jit(solution)/shard_map/sthd,pnhd->sthpn/dot_general | solution.py:188
  162.7 0.8 copy.144
  163.5 1.0 collective-permute-done
  164.7 0.8 slice_bitcast_fusion.3
  165.4 1.5 fusion.64
  167.0 1.6 copy.134
  168.8 1.2 copy.137
  170.0 9.7 %fusion.2 = (bf16[128,8,2,4,384]{0,4,1,3,2:T(8,128)(2,1)}, f32[128,8,2]{0,1,2:T(8,128)S(1)}) fusion(f32[2,4,384,128,8]{3,2,4,1,0:T(8,128)} %get-tuple-element.28, f32[128,8,2]{0,1,2:T(8,128)S(1)} %copy_maximum_fusion, pred[128,4,384]{0,2,1:T(8,128)(4,1)} %broadcast_and_fusion), kind=kLoop, calls=%fused_computation.7 | loop fusion | flops 18872320 | bytes 19087360 | tf_op jit(solution)/shard_map/convert_element_type | solution.py:197
  179.7 0.8 copy.143
  180.5 9.0 %copy.145 = bf16[128,8,2,4,384]{4,1,3,2,0:T(8,128)(2,1)} copy(bf16[128,8,2,4,384]{0,4,1,3,2:T(8,128)(2,1)} %get-tuple-element.9) | data formatting | bytes 12582912 | tf_op jit(solution)/shard_map/convert_element_type | solution.py:197
  189.5 0.8 copy.148
  190.3 1.8 fusion.25
  192.1 1.2 copy-done.1
  193.4 1.9 fusion.33
  195.4 3.2 convolution_convert_fusion
  198.7 2.1 gather_fusion
  201.0 60.2 %reduce-scatter.2.cloned.1.call-done = bf16[1,128,2048]{2,1,0:T(8,128)(2,1)} async-done(((bf16[8,128,2048]{2,1,0:T(8,128)(2,1)}), bf16[1,128,2048]{2,1,0:T(8,128)(2,1)}) %reduce-scatter.2.cloned.1.call-update) | async-done | bytes 524304 | tf_op jit(solution)/shard_map/reduce_scatter | solution.py:212
  261.2 1.5 fusion.34
  262.6 2.7 convolution_convert_fusion.1
  265.4 2.5 reshape.422
  267.9 42.8 %all_to_all.15 = bf16[128,2,2048]{2,1,0:T(2,128)(2,1)} all-to-all(bf16[128,2,2048]{2,1,0:T(2,128)(2,1)} %reshape.422), channel_id=1, replica_groups=mesh['groups'=2,'ep'=16,'rep'=8] {'ep','rep'}, dimensions={0} | all-to-all | bytes 2097152 | tf_op jit(solution)/shard_map/all_to_all | solution.py:246
  310.7 2.2 reshape.423
  312.9 4.1 %fusion.16 = f32[256,768]{1,0:T(8,128)} fusion(bf16[256,2048]{1,0:T(8,128)(2,1)} %reshape.423, bf16[1,2048,768]{2,1,0:T(8,128)(2,1)} %param.24), kind=kOutput, calls=%fused_computation.21 | convolution fusion | flops 805306368 | bytes 4980736 | tf_op jit(solution)/shard_map/dot_general | solution.py:62
  317.0 5.5 %fusion.18 = bf16[256,2048]{1,0:T(8,128)(2,1)} fusion(bf16[1,768,2048]{2,1,0:T(8,128)(2,1)S(1)} %copy-done, bf16[256,2048]{1,0:T(8,128)(2,1)} %reshape.423, bf16[1,2048,768]{2,1,0:T(8,128)(2,1)} %param.25, f32[256,768]{1,0:T(8,128)} %fusion.16), kind=kOutput, calls=%fused_computation.24 | convolution fusion | flops 1612316672 | bytes 9175040 | tf_op jit(solution)/shard_map/dot_general | solution.py:66
  322.5 2.5 reshape.424
  325.1 38.7 %all_to_all.16 = bf16[128,2,2048]{2,1,0:T(2,128)(2,1)} all-to-all(bf16[128,2,2048]{2,1,0:T(2,128)(2,1)} %reshape.424), channel_id=1, replica_groups=mesh['groups'=2,'ep'=16,'rep'=8] {'ep','rep'}, dimensions={0} | all-to-all | bytes 2097152 | tf_op jit(solution)/shard_map/all_to_all | solution.py:251
  363.7 2.2 reshape.425
  366.0 2.7 fusion.22
  (71 shorter events, 2.0 us)
Async XLA Ops:
  6.5 310.5 %copy-start = (bf16[1,768,2048]{2,1,0:T(8,128)(2,1)S(1)}, bf16[1,768,2048]{2,1,0:T(8,128)(2,1)}, u32[]{:S(2)}) copy-start(bf16[1,768,2048]{2,1,0:T(8,128)(2,1)} %param.26) | copy-start | bytes 9437188
  6.6 11.8 %copy-start.2 = (bf16[4,24,2048]{2,1,0:T(8,128)(2,1)S(1)}, bf16[4,24,2048]{2,1,0:T(8,128)(2,1)}, u32[]{:S(2)}) copy-start(bf16[4,24,2048]{2,1,0:T(8,128)(2,1)} %param.17) | copy-start | bytes 1179652
  6.6 12.0 %copy-start.11 = (f32[2048]{0:T(1024)S(1)}, f32[2048]{0:T(1024)}, u32[]{:S(2)}) copy-start(f32[2048]{0:T(1024)} %param.20) | copy-start | bytes 24580
  10.2 11.5 %copy-start.10 = (s32[4]{0:T(128)S(1)}, s32[4]{0:T(128)}, u32[]{:S(2)}) copy-start(s32[4]{0:T(128)} %param.29) | copy-start | bytes 52
  10.2 131.0 %all-to-all-start = ((bf16[8,128,1,2048]{3,1,2,0:T(8,128)(2,1)}), bf16[8,128,1,2048]{3,1,2,0:T(8,128)(2,1)}, u32[]{:S(2)}, u32[]{:S(2)}) async-start(bf16[8,128,1,2048]{3,1,2,0:T(8,128)(2,1)} %stack.2), calls=%async_computation | async-start | bytes 8388608 | tf_op jit(solution)/shard_map/all_to_all | solution.py:88
  18.2 242.9 %reduce-scatter.2.cloned.1.call-start = ((), (), s32[]{:S(2)}) async-start(), calls=%async_computation.4 | async-start | bytes 4718592 | tf_op jit(solution)/shard_map/reduce_scatter | solution.py:212
  18.3 1.9 copy-start.14
  20.3 75.3 %collective-permute-start.1 = (bf16[4,24,128]{2,1,0:T(8,128)(2,1)S(1)}, bf16[4,24,128]{2,1,0:T(8,128)(2,1)S(1)}, u32[]{:S(2)}, u32[]{:S(2)}) collective-permute-start(bf16[4,24,128]{2,1,0:T(8,128)(2,1)S(1)} %fusion.94), channel_id=1, source_target_pairs={{0,1},{1,0},{2,3},{3,2},{4,5},{5,4},{6,7},{7,6},{8,9},{9,8},{10,11... | collective-permute-start | bytes 73736 | tf_op jit(solution)/shard_map/ppermute | solution.py:32
  148.9 5.0 %copy-start.8 = (f32[128,8]{1,0:T(8,128)S(1)}, f32[128,8]{1,0:T(8,128)}, u32[]{:S(2)}) copy-start(f32[128,8]{1,0:T(8,128)} %iota_add_fusion) | copy-start | bytes 12292
  149.0 5.0 %copy-start.15 = (f32[64]{0:T(128)S(1)}, f32[64]{0:T(128)}, u32[]{:S(2)}) copy-start(f32[64]{0:T(128)} %copy-done.14) | copy-start | bytes 772
  149.0 7.9 %copy-start.4 = (pred[128,4,384]{0,2,1:T(8,128)(4,1)S(1)}, pred[128,4,384]{0,2,1:T(8,128)(4,1)}, u32[]{:S(2)}) copy-start(pred[128,4,384]{0,2,1:T(8,128)(4,1)} %broadcast_and_fusion) | copy-start | bytes 589828
  149.0 7.9 %copy-start.5 = (bf16[128,8,256]{2,1,0:T(8,128)(2,1)S(1)}, bf16[128,8,256]{2,1,0:T(8,128)(2,1)}, u32[]{:S(2)}) copy-start(bf16[128,8,256]{2,1,0:T(8,128)(2,1)} %param.19) | copy-start | bytes 1572868
  149.0 7.9 %copy-start.7 = (bf16[4,384,128]{2,1,0:T(8,128)(2,1)S(1)}, bf16[4,384,128]{2,1,0:T(8,128)(2,1)}, u32[]{:S(2)}) copy-start(bf16[4,384,128]{2,1,0:T(8,128)(2,1)} %copy.139) | copy-start | bytes 1179652
  149.0 7.9 %copy-start.16 = (pred[2]{0:T(512)(128)(4,1)S(1)}, pred[2]{0:T(512)(128)(4,1)}, u32[]{:S(2)}) copy-start(pred[2]{0:T(512)(128)(4,1)} %compare_and_fusion) | copy-start | bytes 10
  156.5 8.0 %collective-permute-start = (bf16[128,8,128]{2,1,0:T(8,128)(2,1)S(1)}, bf16[128,8,128]{2,1,0:T(8,128)(2,1)S(1)}, u32[]{:S(2)}, u32[]{:S(2)}) collective-permute-start(bf16[128,8,128]{2,1,0:T(8,128)(2,1)S(1)} %fusion.61), channel_id=1, source_target_pairs={{0,1},{1,0},{2,3},{3,2},{4,5},{5,4},{6,7},{7,6},{8,9},{9,8},{10,11... | collective-permute-start | bytes 786440 | tf_op jit(solution)/shard_map/ppermute | solution.py:32
  156.9 11.7 %copy-start.13 = (pred[8,8]{1,0:T(8,128)(4,1)S(1)}, pred[8,8]{1,0:T(8,128)(4,1)}, u32[]{:S(2)}) copy-start(pred[8,8]{1,0:T(8,128)(4,1)} %iota_compare_fusion.5) | copy-start | bytes 196
  180.5 9.8 %copy-start.17 = (pred[2]{0:T(512)(128)(4,1)S(1)}, pred[2]{0:T(512)(128)(4,1)}, u32[]{:S(2)}) copy-start(pred[2]{0:T(512)(128)(4,1)} %compare_and_fusion) | copy-start | bytes 10
  189.5 2.6 copy-start.6
  190.3 3.1 copy-start.1
  190.3 3.1 copy-start.9
  193.4 1.9 copy-start.3
  195.3 3.3 copy-start.18
  195.3 67.3 %copy-start.12 = (f32[2048]{0:T(1024)S(1)}, f32[2048]{0:T(1024)}, u32[]{:S(2)}) copy-start(f32[2048]{0:T(1024)} %param.23) | copy-start | bytes 24580
Sparse Core Ops, SparseCore 0:
  198.8 62.3 reduce-scatter.1
